TPU v7x, 16 devices: a 4x2x1 block of a 4x4x8 slice. The times are simulated.
16 devices in a mesh: dp: 2 (over y, z), ep: 8 (over x, core).
Axes of the slice: x: 4, y: 2, z: 1, core: 2. Of those that a mesh axis runs over, the one named last changes fastest.
The devices are a block of a 4x4x8 slice.
Arguments:
- x: bfloat16 [16384, 2048], P(('dp', 'ep')), parts along dimension 0
- route_idx: int32 [16384, 4], P(('dp', 'ep')), parts along dimension 0
- route_gate: float32 [16384, 4], P(('dp', 'ep')), parts along dimension 0
- w_gate: bfloat16 [8, 2048, 1408], P('ep')
- w_up: bfloat16 [8, 2048, 1408], P('ep')
- w_down: bfloat16 [8, 1408, 2048], P('ep')
- grad_y: bfloat16 [16384, 2048], P(('dp', 'ep')), parts along dimension 0
Outputs:
- output 1: bfloat16 [16384, 2048], P(('dp', 'ep')), parts along dimension 0
- output 2: bfloat16 [16384, 2048], P(('dp', 'ep')), parts along dimension 0
- output 3: bfloat16 [16, 2048, 1408], P(('dp', 'ep')), parts along dimension 0
- output 4: bfloat16 [16, 2048, 1408], P(('dp', 'ep')), parts along dimension 0
- output 5: bfloat16 [16, 1408, 2048], P(('dp', 'ep')), parts along dimension 0
There are 2 independent parts. A program takes and returns all parts, laid end to end along the dimension named above; an argument that names none is the same for every part.
All inputs are finite; a program needn't handle non-finite values.
Results may differ from a plain program's by a relative error of at most 0.00155.
Values are sent between devices in bfloat16 or wider.
A program may use at most 768 MiB of HBM per device.

v0:
```python
import jax
import jax.numpy as jnp
from jax import lax
from jax.sharding import PartitionSpec as P


def pack_plan(route_loc, n_dest, capacity):
    tok_count, top_k = route_loc.shape
    flat_dest = route_loc.reshape(tok_count * top_k)
    hits = (flat_dest[:, None] == jnp.arange(n_dest, dtype=jnp.int32)[None, :]).astype(jnp.int32)
    slot_rank = jnp.sum((jnp.cumsum(hits, axis=0) - hits) * hits, axis=1)
    slot_pos = flat_dest * capacity + slot_rank
    slot_tok = jnp.arange(tok_count * top_k, dtype=jnp.int32) // top_k
    src_tok = jnp.zeros((n_dest * capacity,), jnp.int32).at[slot_pos].set(slot_tok)
    filled = jnp.zeros((n_dest * capacity,), jnp.bool_).at[slot_pos].set(True)
    return slot_pos, src_tok, filled


def expert_forward(rows, gate_mat, up_mat, down_mat):
    pre_gate = jnp.dot(rows, gate_mat, preferred_element_type=jnp.float32)
    pre_up = jnp.dot(rows, up_mat, preferred_element_type=jnp.float32)
    sig_gate = jax.nn.sigmoid(pre_gate)
    hidden = (pre_gate * sig_gate * pre_up).astype(jnp.bfloat16)
    expert_out = jnp.dot(hidden, down_mat, preferred_element_type=jnp.float32).astype(jnp.bfloat16)
    return expert_out, pre_gate, pre_up, hidden


def expert_backward(rows, out_cot, pre_gate, pre_up, hidden, gate_mat, up_mat, down_mat):
    contract_last = (((1,), (1,)), ((), ()))
    contract_first = (((0,), (0,)), ((), ()))
    sig_gate = jax.nn.sigmoid(pre_gate)
    grad_hidden = lax.dot_general(out_cot, down_mat, contract_last, preferred_element_type=jnp.float32).astype(jnp.bfloat16).astype(jnp.float32)
    grad_gate = (grad_hidden * pre_up * (sig_gate * (1.0 + pre_gate * (1.0 - sig_gate)))).astype(jnp.bfloat16)
    grad_up = (grad_hidden * (pre_gate * sig_gate)).astype(jnp.bfloat16)
    grad_rows = (lax.dot_general(grad_gate, gate_mat, contract_last, preferred_element_type=jnp.float32) + lax.dot_general(grad_up, up_mat, contract_last, preferred_element_type=jnp.float32)).astype(jnp.bfloat16)
    grad_gate_mat = lax.dot_general(rows, grad_gate, contract_first, preferred_element_type=jnp.float32).astype(jnp.bfloat16)
    grad_up_mat = lax.dot_general(rows, grad_up, contract_first, preferred_element_type=jnp.float32).astype(jnp.bfloat16)
    grad_down_mat = lax.dot_general(hidden, out_cot, contract_first, preferred_element_type=jnp.float32).astype(jnp.bfloat16)
    return grad_rows, grad_gate_mat, grad_up_mat, grad_down_mat


def solution(mesh):
    n_exp = mesh.shape["ep"]
    row_spec = P(("dp", "ep"), None)
    weight_spec = P("ep", None, None)
    grad_w_spec = P(("dp", "ep"), None, None)

    def local(x, route_idx, route_gate, w_gate, w_up, w_down, grad_y):
        tok_count, d_model = x.shape
        top_k = route_idx.shape[1]
        capacity = 3 * tok_count // 4
        gate_mat, up_mat, down_mat = w_gate[0], w_up[0], w_down[0]
        slot_pos, src_tok, filled = pack_plan(route_idx, n_exp, capacity)
        gate_buf = jnp.zeros((n_exp * capacity,), jnp.float32).at[slot_pos].set(route_gate.reshape(tok_count * top_k))
        send_rows = jnp.where(filled[:, None], jnp.take(x, src_tok, axis=0), 0)
        recv_rows = lax.all_to_all(send_rows, "ep", 0, 0, tiled=True)
        expert_out, pre_gate, pre_up, hidden = expert_forward(recv_rows, gate_mat, up_mat, down_mat)
        back_out = lax.all_to_all(expert_out, "ep", 0, 0, tiled=True)
        slot_out = jnp.take(back_out, slot_pos, axis=0).reshape(tok_count, top_k, d_model)
        y = jnp.sum(route_gate[:, :, None] * slot_out.astype(jnp.float32), axis=1).astype(jnp.bfloat16)
        send_cot = (gate_buf[:, None] * jnp.take(grad_y, src_tok, axis=0).astype(jnp.float32)).astype(jnp.bfloat16)
        recv_cot = lax.all_to_all(send_cot, "ep", 0, 0, tiled=True)
        grad_rows, grad_gate_mat, grad_up_mat, grad_down_mat = expert_backward(recv_rows, recv_cot, pre_gate, pre_up, hidden, gate_mat, up_mat, down_mat)
        back_grad = lax.all_to_all(grad_rows, "ep", 0, 0, tiled=True)
        slot_grad = jnp.take(back_grad, slot_pos, axis=0).reshape(tok_count, top_k, d_model)
        grad_x = jnp.sum(slot_grad.astype(jnp.float32), axis=1).astype(jnp.bfloat16)
        return y, grad_x, grad_gate_mat[None], grad_up_mat[None], grad_down_mat[None]

    return jax.shard_map(local, mesh=mesh, in_specs=(row_spec, row_spec, row_spec, weight_spec, weight_spec, weight_spec, row_spec), out_specs=(row_spec, row_spec, grad_w_spec, grad_w_spec, grad_w_spec), check_vma=False)
```

profile of v0, /device:TPU:112, one launch (start us, length us, event | category | flops | bytes accessed | tf_op | source)
XLA Modules:
  0.0 1578.3 jit_solution(18239819619390142761)
XLA Ops:
  0.6 0.7 broadcast_multiply_fusion
  1.4 0.9 copy.14
  2.3 0.3 eq.25
  2.6 0.3 eq.29
  2.9 0.2 copy.16
  3.1 0.3 mul.64
  3.5 2.3 reduce-window.6
  5.8 0.3 slice_reduce_fusion
  6.1 0.2 reduce-window.9
  6.3 0.1 add_bitcast_fusion
  6.4 0.1 fusion.18
  6.5 0.0 copy-start.4
  6.5 0.6 copy-done.4
  7.1 15.5 scatter_custom_fusion.1
  22.7 0.9 copy.13
  23.7 0.0 copy-start
  23.7 0.3 reshape.142
  24.0 15.5 scatter_custom_fusion.2
  39.5 49.1 %gather_fusion.2 = bf16[6144,2048]{1,0:T(8,128)(2,1)} fusion(bf16[1024,2048]{1,0:T(8,128)(2,1)} %param.17, s32[6144]{0:T(1024)S(1)} %fusion.20), kind=kCustom, calls=%fused_computation.2.clone | custom fusion | bytes 50356224 | tf_op jit(solution)/shard_map/jit(_take)/gather | solution.py:61
  88.6 22.8 %multiply_convert_fusion = bf16[6144,2048]{1,0:T(8,128)(2,1)} fusion(bf16[6144,2048]{1,0:T(8,128)(2,1)} %gather_fusion.2, f32[6144]{0:T(1024)S(1)} %scatter_custom_fusion.2, pred[6144]{0:T(1024)(128)(4,1)S(1)} %compare_and_fusion), kind=kLoop, calls=%fused_computation.8 | loop fusion | flops 50331648 | bytes 50362368 | tf_op jit(solution)/shard_map/convert_element_type | solution.py:61
  111.4 6.9 all-to-all-start.2
  118.3 49.1 %gather_fusion = bf16[6144,2048]{1,0:T(8,128)(2,1)} fusion(bf16[1024,2048]{1,0:T(8,128)(2,1)} %param.11, s32[6144]{0:T(1024)S(1)} %fusion.20), kind=kCustom, calls=%fused_computation.clone | custom fusion | bytes 50356224 | tf_op jit(solution)/shard_map/jit(_take)/gather | solution.py:55
  167.3 17.7 %scatter_custom_fusion = pred[6144]{0:T(1024)(128)(4,1)S(1)} fusion(s32[4096]{0:T(1024)} %bitcast.75, pred[4096]{0:T(1024)(128)(4,1)S(1)} %broadcast.70, pred[]{:T(512)} %constant.32.clone.1), kind=kCustom, calls=%fused_computation.64 | custom fusion | bytes 6656 | tf_op jit(solution)/shard_map/scatter | solution.py:15
  185.1 22.2 %select_select_fusion = bf16[6144,2048]{1,0:T(8,128)(2,1)} fusion(bf16[6144,2048]{1,0:T(8,128)(2,1)} %gather_fusion, pred[6144]{0:T(1024)(128)(4,1)S(1)} %compare_and_fusion, pred[6144]{0:T(1024)(128)(4,1)S(1)} %scatter_custom_fusion), kind=kLoop, calls=%fused_computation.18 | loop fusion | flops 25165824 | bytes 50343936 | tf_op jit(solution)/shard_map/jit(_where)/select_n | solution.py:55
  207.3 185.4 %all-to-all-done.2 = bf16[8,768,2048]{2,1,0:T(8,128)(2,1)} async-done(((bf16[8,768,2048]{2,1,0:T(8,128)(2,1)}), bf16[8,768,2048]{2,1,0:T(8,128)(2,1)}, u32[]{:S(2)}, u32[]{:S(2)}) %all-to-all-start.2) | async-done | bytes 25165856 | tf_op jit(solution)/shard_map/all_to_all | solution.py:62
  392.7 7.1 all-to-all-start
  399.8 45.7 %convolution_convert_fusion = bf16[6144,1408]{1,0:T(8,128)(2,1)} fusion(bf16[6144,2048]{1,0:T(8,128)(2,1)} %bitcast.11, bf16[1,1408,2048]{2,1,0:T(8,128)(2,1)} %param.16), kind=kOutput, calls=%fused_computation.19 | convolution fusion | flops 35442130944 | bytes 48234496 | tf_op jit(solution)/shard_map/dot_general | solution.py:32
  445.6 228.4 %all-to-all-done = bf16[8,768,2048]{2,1,0:T(8,128)(2,1)} async-done(((bf16[8,768,2048]{2,1,0:T(8,128)(2,1)}), bf16[8,768,2048]{2,1,0:T(8,128)(2,1)}, u32[]{:S(2)}, u32[]{:S(2)}) %all-to-all-start) | async-done | bytes 25165856 | tf_op jit(solution)/shard_map/all_to_all | solution.py:56
  674.0 46.3 %fusion.14 = f32[6144,1408]{1,0:T(8,128)} fusion(bf16[6144,2048]{1,0:T(8,128)(2,1)} %bitcast.4, bf16[1,2048,1408]{2,1,0:T(8,128)(2,1)} %param.14), kind=kOutput, calls=%fused_computation.36 | convolution fusion | flops 35433480192 | bytes 65536000 | tf_op jit(solution)/shard_map/dot_general | solution.py:20
  720.3 62.3 %fusion.1 = (bf16[6144,1408]{1,0:T(8,128)(2,1)}, bf16[6144,1408]{1,0:T(8,128)(2,1)}, bf16[6144,1408]{1,0:T(8,128)(2,1)}) fusion(bf16[6144,1408]{1,0:T(8,128)(2,1)} %convolution_convert_fusion, f32[6144,1408]{1,0:T(8,128)} %fusion.14, bf16[6144,2048]{1,0:T(8,128)(2,1)} %bitcast.4, bf16[1,2048,1408]{2,1,0:T(8,128)(2,1)} %param.15), kind=kOutput, calls=%fused_computation.12 | convolution fusion | flops 35571892224 | bytes 134742016 | tf_op jit(solution)/shard_map/dot_general | solution.py:21
  782.6 45.5 %convolution_convert_fusion.1 = bf16[6144,2048]{1,0:T(8,128)(2,1)} fusion(bf16[6144,1408]{1,0:T(8,128)(2,1)} %get-tuple-element.8, bf16[1,1408,2048]{2,1,0:T(8,128)(2,1)} %param.16), kind=kOutput, calls=%fused_computation.20 | convolution fusion | flops 35446063104 | bytes 48234496 | tf_op jit(solution)/shard_map/dot_general | solution.py:24
  828.1 6.8 all-to-all-start.1
  834.9 46.9 %fusion.12 = f32[6144,2048]{1,0:T(8,128)} fusion(bf16[6144,1408]{1,0:T(8,128)(2,1)} %get-tuple-element.7, bf16[1,2048,1408]{2,1,0:T(8,128)(2,1)} %param.14), kind=kOutput, calls=%fused_computation.34 | convolution fusion | flops 35433480192 | bytes 73400320 | tf_op jit(solution)/shard_map/dot_general | solution.py:35
  881.8 48.1 %add_convert_fusion = bf16[6144,2048]{1,0:T(8,128)(2,1)} fusion(f32[6144,2048]{1,0:T(8,128)} %fusion.12, bf16[6144,1408]{1,0:T(8,128)(2,1)} %get-tuple-element.9, bf16[1,2048,1408]{2,1,0:T(8,128)(2,1)} %param.15), kind=kOutput, calls=%fused_computation.7 | convolution fusion | flops 35458646016 | bytes 98566144 | tf_op jit(solution)/shard_map/dot_general | solution.py:35
  929.8 179.2 %all-to-all-done.1 = bf16[8,768,2048]{2,1,0:T(8,128)(2,1)} async-done(((bf16[8,768,2048]{2,1,0:T(8,128)(2,1)}), bf16[8,768,2048]{2,1,0:T(8,128)(2,1)}, u32[]{:S(2)}, u32[]{:S(2)}) %all-to-all-start.1) | async-done | bytes 25165856 | tf_op jit(solution)/shard_map/all_to_all | solution.py:58
  1109.0 7.0 all-to-all-start.3
  1116.1 0.6 compare_and_fusion.1
  1116.7 45.5 %fusion.6 = bf16[1,1408,2048]{2,1,0:T(8,128)(2,1)} fusion(bf16[6144,1408]{1,0:T(8,128)(2,1)} %get-tuple-element.8, bf16[6144,2048]{1,0:T(8,128)(2,1)} %bitcast.11), kind=kOutput, calls=%fused_computation.28 | convolution fusion | flops 35436363776 | bytes 48234496 | tf_op jit(solution)/shard_map/dot_general | solution.py:38
  1162.2 49.4 %fusion.4 = bf16[1,2048,1408]{2,1,0:T(8,128)(2,1)} fusion(bf16[6144,2048]{1,0:T(8,128)(2,1)} %bitcast.4, bf16[6144,1408]{1,0:T(8,128)(2,1)} %get-tuple-element.7), kind=kOutput, calls=%fused_computation.26 | convolution fusion | flops 35436363776 | bytes 48234496 | tf_op jit(solution)/shard_map/dot_general | solution.py:36
  1211.6 49.1 %fusion.5 = bf16[1,2048,1408]{2,1,0:T(8,128)(2,1)} fusion(bf16[6144,2048]{1,0:T(8,128)(2,1)} %bitcast.4, bf16[6144,1408]{1,0:T(8,128)(2,1)} %get-tuple-element.9), kind=kOutput, calls=%fused_computation.27 | convolution fusion | flops 35436363776 | bytes 48234496 | tf_op jit(solution)/shard_map/dot_general | solution.py:37
  1260.7 42.9 %gather_fusion.1 = bf16[4096,2048]{1,0:T(8,128)(2,1)} fusion(bf16[6144,2048]{1,0:T(8,128)(2,1)} %bitcast.9, s32[4096]{0:T(1024)S(1)} %broadcast_clamp_fusion), kind=kCustom, calls=%fused_computation.1.clone | custom fusion | bytes 33570816 | tf_op jit(solution)/shard_map/jit(_take)/gather | solution.py:59
  1303.6 86.6 %all-to-all-done.3 = bf16[8,768,2048]{2,1,0:T(8,128)(2,1)} async-done(((bf16[8,768,2048]{2,1,0:T(8,128)(2,1)}), bf16[8,768,2048]{2,1,0:T(8,128)(2,1)}, u32[]{:S(2)}, u32[]{:S(2)}) %all-to-all-start.3) | async-done | bytes 25165856 | tf_op jit(solution)/shard_map/all_to_all | solution.py:64
  1390.2 42.7 %gather_fusion.3 = bf16[4096,2048]{1,0:T(8,128)(2,1)} fusion(bf16[6144,2048]{1,0:T(8,128)(2,1)} %bitcast.13, s32[4096]{0:T(1024)S(1)} %broadcast_clamp_fusion), kind=kCustom, calls=%fused_computation.3.clone | custom fusion | bytes 33570816 | tf_op jit(solution)/shard_map/jit(_take)/gather | solution.py:65
  1432.9 29.2 %broadcast_select_fusion = (bf16[4096,2048]{1,0:T(8,128)(2,1)}, f32[4096,2048]{1,0:T(8,128)}) fusion(bf16[4096,2048]{1,0:T(8,128)(2,1)} %gather_fusion.3, pred[4096]{0:T(1024)(128)(4,1)S(1)} %copy-done.7, bf16[4096,2048]{1,0:T(8,128)(2,1)} %gather_fusion.1), kind=kLoop, calls=%fused_computation.22 | loop fusion | flops 25165824 | bytes 83890176 | tf_op jit(solution)/shard_map/jit(_take)/select_n | solution.py:65
  1462.2 24.8 %reshape.88 = bf16[1024,4,2048]{2,1,0:T(4,128)(2,1)} reshape(bf16[4096,2048]{1,0:T(8,128)(2,1)} %get-tuple-element.10) | data formatting | bytes 33554432 | tf_op jit(solution)/shard_map/reshape | solution.py:65
  1487.0 37.4 %reshape.89 = f32[1024,4,2048]{2,1,0:T(4,128)} reshape(f32[4096,2048]{1,0:T(8,128)} %get-tuple-element.11) | data formatting | bytes 67108864 | tf_op jit(solution)/shard_map/convert_element_type | solution.py:60
  1524.5 28.9 %multiply_reduce_fusion = bf16[1024,2048]{1,0:T(8,128)(2,1)} fusion(f32[1024,4,2048]{2,1,0:T(4,128)} %reshape.89, f32[1024,4]{1,0:T(8,128)S(1)} %copy-done.1), kind=kLoop, calls=%fused_computation.17 | loop fusion | flops 14680064 | bytes 37765120 | tf_op jit(solution)/shard_map/reduce_sum | solution.py:60
  1553.3 24.7 %reduce_sum.35 = bf16[1024,2048]{1,0:T(8,128)(2,1)} reduce(bf16[1024,4,2048]{2,1,0:T(4,128)(2,1)} %reshape.88, bf16[]{:T(256)} %constant.58.clone.1), dimensions={1}, to_apply=%region_7.10 | reduce | flops 6291456 | bytes 20971522 | tf_op jit(solution)/shard_map/reduce_sum | solution.py:66
  (20 shorter events, 0.1 us)
Async XLA Ops:
  2.6 86.0 %copy-start.2 = (s32[4096]{0:T(1024)}, s32[4096]{0:T(1024)S(1)}, u32[]{:S(2)}) copy-start(s32[4096]{0:T(1024)S(1)} %eq.25) | copy-start | bytes 49156
  6.5 0.6 copy-start.4
  7.1 81.5 %copy-start.6 = (s32[4096,1]{0,1:T(1,128)}, s32[4096,1]{0,1:T(1,128)S(1)}, u32[]{:S(2)}) copy-start(s32[4096,1]{0,1:T(1,128)S(1)} %compare_select_fusion) | copy-start | bytes 49156
  23.7 64.9 %copy-start = (f32[1024,4]{1,0:T(8,128)}, f32[1024,4]{1,0:T(8,128)S(1)}, u32[]{:S(2)}) copy-start(f32[1024,4]{1,0:T(8,128)S(1)} %copy.13) | copy-start | bytes 49156
  111.4 281.3 %all-to-all-start.2 = ((bf16[8,768,2048]{2,1,0:T(8,128)(2,1)}), bf16[8,768,2048]{2,1,0:T(8,128)(2,1)}, u32[]{:S(2)}, u32[]{:S(2)}) async-start(bf16[8,768,2048]{2,1,0:T(8,128)(2,1)} %bitcast.67), calls=%async_computation.2 | async-start | bytes 50331648 | tf_op jit(solution)/shard_map/all_to_all | solution.py:62
  392.7 281.3 %all-to-all-start = ((bf16[8,768,2048]{2,1,0:T(8,128)(2,1)}), bf16[8,768,2048]{2,1,0:T(8,128)(2,1)}, u32[]{:S(2)}, u32[]{:S(2)}) async-start(bf16[8,768,2048]{2,1,0:T(8,128)(2,1)} %bitcast.68), calls=%async_computation | async-start | bytes 50331648 | tf_op jit(solution)/shard_map/all_to_all | solution.py:56
  828.1 281.0 %all-to-all-start.1 = ((bf16[8,768,2048]{2,1,0:T(8,128)(2,1)}), bf16[8,768,2048]{2,1,0:T(8,128)(2,1)}, u32[]{:S(2)}, u32[]{:S(2)}) async-start(bf16[8,768,2048]{2,1,0:T(8,128)(2,1)} %bitcast.70), calls=%async_computation.1 | async-start | bytes 50331648 | tf_op jit(solution)/shard_map/all_to_all | solution.py:58
  1109.0 7.0 copy-start.3
  1109.0 7.0 copy-start.5
  1109.0 281.2 %all-to-all-start.3 = ((bf16[8,768,2048]{2,1,0:T(8,128)(2,1)}), bf16[8,768,2048]{2,1,0:T(8,128)(2,1)}, u32[]{:S(2)}, u32[]{:S(2)}) async-start(bf16[8,768,2048]{2,1,0:T(8,128)(2,1)} %bitcast.69), calls=%async_computation.3 | async-start | bytes 50331648 | tf_op jit(solution)/shard_map/all_to_all | solution.py:64
  1390.2 42.7 %copy-start.7 = (pred[4096]{0:T(1024)(128)(4,1)S(1)}, pred[4096]{0:T(1024)(128)(4,1)}, u32[]{:S(2)}) copy-start(pred[4096]{0:T(1024)(128)(4,1)} %compare_and_fusion.1) | copy-start | bytes 12292
  1487.0 37.4 %copy-start.1 = (f32[1024,4]{1,0:T(8,128)S(1)}, f32[1024,4]{1,0:T(8,128)}, u32[]{:S(2)}) copy-start(f32[1024,4]{1,0:T(8,128)} %copy-done) | copy-start | bytes 49156
where the time goes:
time: 1590 us; the launch traced here: 1580 us
  waiting for transfers between devices  680 us (43%)
  matrix products  439 us (28%)
  local copies, waits for them, and re-layouts  299 us (19%)
  other arithmetic  132 us (8%)
  starting transfers between devices  27.8 us (2%)
    all_to_all x1, waiting for transfers between devices, local(): recv_rows = lax.all_to_all(send_rows, 'ep', 0, 0, tiled=True)  228 us
    all_to_all x1, waiting for transfers between devices, local(): recv_cot = lax.all_to_all(send_cot, 'ep', 0, 0, tiled=True)  185 us
    all_to_all x1, waiting for transfers between devices, local(): back_out = lax.all_to_all(expert_out, 'ep', 0, 0, tiled=True)  179 us
    all_to_all x1, waiting for transfers between devices, local(): back_grad = lax.all_to_all(grad_rows, 'ep', 0, 0, tiled=True)  86.6 us
    dot_general x1, matrix products, expert_forward(): pre_up = jnp.dot(rows, up_mat, preferred_element_type=jnp.float32)  62.3 us
    dot_general x1, matrix products, expert_backward(): lax.dot_general(rows, grad_gate, contract_first, preferred_element_type=j...  49.4 us
    dot_general x1, matrix products, expert_backward(): lax.dot_general(rows, grad_up, contract_first, preferred_element_type=jnp...  49.1 us
    gather x1, local copies, waits for them, and re-layouts, local(): jnp.take(grad_y, src_tok, axis=0).astype(jnp.float32)  49.1 us
  transfers between devices with their start and end apart: 4, of which 4 were waited for; matrix products, arithmetic and copies ran while one was open for 26% of the time, Pallas kernels for 0%

commit v1 on v0

v1 whole, which is shorter than its diff:
```python
import functools

import jax
import jax.numpy as jnp
from jax import lax
from jax.experimental import pallas as pl
from jax.experimental.pallas import tpu as pltpu
from jax.sharding import PartitionSpec as P

MESH = pl.DeviceIdType.MESH
MID = (((1,), (0,)), ((), ()))
LAST = (((1,), (1,)), ((), ()))
FIRST = (((0,), (0,)), ((), ()))
BF = jnp.bfloat16
F32 = jnp.float32


def dot(a, b, dims=MID):
    return lax.dot_general(a, b, dims, preferred_element_type=F32)


def layer_kernel(n, cap, x_ref, gy_ref, meta_ref, wg_ref, wu_ref, wd_ref,
                 xr_out, a_out, b_out, h_out, o_out, c_out, da_out, db_out, r_out, back_o, xg, gyg, mg,
                 wg, wu, wd, xbuf, mbuf, tri, pbuf, posbuf, xr, ab_a, ab_b, hb, ob, cb, dab, dbb,
                 send_sem, recv_sem, osend_sem, orecv_sem, wsem, lsem, outsem):
    tok, d = x_ref.shape
    ff = wd_ref.shape[1]
    half = tok // 2
    me = lax.axis_index("ep")
    chips = n // 2
    chip, core = me // 2, lax.rem(me, 2)
    right = lax.rem(chip + 1, chips) * 2 + core
    left = lax.rem(chip + chips - 1, chips) * 2 + core
    across = lax.rem(chip + 2, chips) * 2 + core
    mate = chip * 2 + 1 - core
    right_m = lax.rem(chip + 1, chips) * 2 + 1 - core
    left_m = lax.rem(chip + chips - 1, chips) * 2 + 1 - core
    across_m = lax.rem(chip + 2, chips) * 2 + 1 - core
    order = (me, mate, left, right, left_m, right_m, across, across_m)

    barrier = pltpu.get_barrier_semaphore()
    for peer in order[1:]:
        pl.semaphore_signal(barrier, inc=1, device_id={"ep": peer}, device_id_type=MESH)
    pl.semaphore_wait(barrier, n - 1)

    own = (x_ref, gy_ref, meta_ref)
    got = (xg, gyg, mg)

    def part(item, slot, which):
        if item == 2 or which is None:
            return got[item].at[slot]
        return got[item].at[slot, pl.ds(which * half, half)]

    def send(item, k):
        src, dst, peer = {
            0: (own[item], part(item, me, None), right),
            1: (own[item], part(item, me, None), left),
            2: (own[item], part(item, me, None), mate),
            3: (part(item, left, 0), part(item, left, 0), right),
            4: (part(item, right, 1), part(item, right, 1), left),
            5: (part(item, left, None), part(item, left, None), mate),
            6: (part(item, right, None), part(item, right, None), mate),
            7: (part(item, across, None), part(item, across, None), mate),
        }[k]
        return pltpu.make_async_remote_copy(
            src_ref=src, dst_ref=dst, send_sem=send_sem.at[item, k], recv_sem=recv_sem.at[item, k],
            device_id={"ep": peer}, device_id_type=MESH)

    def land(item, k):
        ref = {
            0: part(item, left, None), 1: part(item, right, None), 2: part(item, mate, None),
            3: part(item, across, 0), 4: part(item, across, 1),
            5: part(item, left_m, None), 6: part(item, right_m, None), 7: part(item, across_m, None),
        }[k]
        pltpu.make_async_remote_copy(
            src_ref=ref, dst_ref=ref, send_sem=send_sem.at[item, k], recv_sem=recv_sem.at[item, k],
            device_id={"ep": mate}, device_id_type=MESH).wait_recv()

    def give(j):
        to = order[j]
        return pltpu.make_async_remote_copy(
            src_ref=o_out.at[rows_of(to)], dst_ref=back_o.at[rows_of(me)], send_sem=osend_sem.at[j], recv_sem=orecv_sem.at[me],
            device_id={"ep": to}, device_id_type=MESH)

    def taken(j):
        ref = back_o.at[rows_of(order[j])]
        pltpu.make_async_remote_copy(
            src_ref=ref, dst_ref=ref, send_sem=osend_sem.at[j], recv_sem=orecv_sem.at[order[j]],
            device_id={"ep": mate}, device_id_type=MESH).wait_recv()

    for k in (0, 1, 2):
        send(2, k).start()
    for k in (0, 1, 2):
        send(0, k).start()
    send(1, 2).start()

    weights = [pltpu.make_async_copy(s.at[0], t, wsem.at[q]) for q, (s, t) in enumerate(((wg_ref, wg), (wu_ref, wu), (wd_ref, wd)))]
    for cp in weights:
        cp.start()
    for q in range(4):
        rows = lax.broadcasted_iota(jnp.int32, (tok // 4, tok), 0) + q * (tok // 4)
        cols = lax.broadcasted_iota(jnp.int32, (tok // 4, tok), 1)
        tri[pl.ds(q * (tok // 4), tok // 4), :] = jnp.where(rows <= cols, 1.0, 0.0).astype(BF)
    for cp in weights:
        cp.wait()

    def is_forward(i):
        return (i < 2) | ((i >= 4) & (i < 10))

    def slot_of(i):
        j = jnp.where(i < 2, i, jnp.where(i < 10, i - 2, i - 8))
        hop = jnp.where(j < 2, 0, jnp.where(j >= 6, 2, jnp.where(lax.rem(j, 2) == 0, chips - 1, 1)))
        flip = (j == 1) | (j == 4) | (j == 5) | (j == 7)
        return j, lax.rem(chip + hop, chips) * 2 + jnp.where(flip, 1 - core, core)

    def rows_of(slot):
        return pl.ds(pl.multiple_of(slot * cap, cap), cap)

    f_bufs = ((xr, xr_out), (ab_a, a_out), (ab_b, b_out), (hb, h_out), (ob, o_out))
    b_bufs = ((cb, c_out), (dab, da_out), (dbb, db_out), (ob, r_out))

    def out_copy(q, bufs, slot):
        src, dst = bufs[q]
        return pltpu.make_async_copy(src, dst.at[rows_of(slot)], outsem.at[q + (5 if bufs is b_bufs else 0)])

    def col_tiles(body):
        wide = ff // 256

        def run(t, c):
            body(pl.ds(pl.multiple_of(t * 256, 256), 256))
            return c

        lax.fori_loop(0, wide, run, 0)
        if ff % 256:
            body(pl.ds(wide * 256, ff % 256))

    def model_tiles(body):
        def run(t, c):
            body(pl.ds(pl.multiple_of(t * 512, 512), 512))
            return c

        lax.fori_loop(0, d // 512, run, 0)

    def settle(i):
        last = i - 1

        @pl.when((i > 0) & is_forward(last))
        def _():
            for q in range(5):
                out_copy(q, f_bufs, 0).wait()

        @pl.when((i > 0) & jnp.logical_not(is_forward(last)))
        def _():
            for q in range(4):
                out_copy(q, b_bufs, 0).wait()

        for when, js in ((2, (1,)), (9, (2, 3, 4, 5, 6)), (10, (7,))):
            @pl.when(i == when)
            def _(js=js):
                for j in js:
                    give(j).start()

    def step(i, carry):
        is_f = is_forward(i)
        j, slot = slot_of(i)

        @pl.when(i == 1)
        def _():
            land(0, 2)
            land(2, 2)

        @pl.when(i == 3)
        def _():
            land(1, 2)

        @pl.when(i == 4)
        def _():
            for k in (0, 1):
                land(2, k)
                land(0, k)
            for k in (3, 5, 6):
                send(2, k).start()
            for k in (3, 4, 5, 6):
                send(0, k).start()
            for k in (0, 1):
                send(1, k).start()

        @pl.when(i == 6)
        def _():
            for k in (5, 6):
                land(0, k)
                land(2, k)

        @pl.when(i == 8)
        def _():
            land(2, 3)
            land(0, 3)
            land(0, 4)
            send(2, 7).start()
            send(0, 7).start()

        @pl.when(i == 9)
        def _():
            land(2, 7)
            land(0, 7)
            land(1, 0)
            land(1, 1)
            for k in (3, 4, 5, 6):
                send(1, k).start()

        @pl.when(i == 12)
        def _():
            land(1, 5)
            land(1, 6)

        @pl.when(i == 14)
        def _():
            land(1, 3)
            land(1, 4)
            send(1, 7).start()

        @pl.when(i == 15)
        def _():
            land(1, 7)

        def fetch(own_ref, got_ref, buf, sem):
            @pl.when(j == 0)
            def _():
                pltpu.make_async_copy(own_ref, buf, sem).start()

            @pl.when(j > 0)
            def _():
                pltpu.make_async_copy(got_ref.at[slot], buf, sem).start()

        def fetched(own_ref, buf, sem):
            pltpu.make_async_copy(own_ref, buf, sem).wait()

        fetch(meta_ref, mg, mbuf, lsem.at[1])
        fetched(meta_ref, mbuf, lsem.at[1])
        sel = mbuf[0:4, :] == me.astype(F32)
        gate = jnp.sum(jnp.where(sel, mbuf[4:8, :], 0.0), axis=0, keepdims=True)

        def fill_p():
            pos = posbuf[j][0:1, :]
            for q in range(cap // 128):
                rows = lax.broadcasted_iota(jnp.int32, (128, tok), 0) + q * 128
                pbuf[pl.ds(q * 128, 128), :] = jnp.where(rows == pos, 1.0, 0.0).astype(BF)

        @pl.when(is_f)
        def _():
            fetch(x_ref, xg, xbuf, lsem.at[0])
            hit = jnp.max(jnp.where(sel, 1.0, 0.0), axis=0, keepdims=True)
            count = dot(jnp.broadcast_to(hit, (16, tok)).astype(BF), tri[...])[0:1, :]
            pos = jnp.where(hit > 0.0, count - 1.0, -1.0).astype(jnp.int32)
            posbuf[j] = jnp.broadcast_to(pos, (8, tok))
            fill_p()
            settle(i)
            fetched(x_ref, xbuf, lsem.at[0])

            def pick(cols):
                xr[:, cols] = dot(pbuf[...], xbuf[:, cols]).astype(BF)

            model_tiles(pick)
            out_copy(0, f_bufs, slot).start()

            def up(cols):
                a, b = dot(xr[...], wg[:, cols]), dot(xr[...], wu[:, cols])
                ab_a[:, cols] = a
                ab_b[:, cols] = b
                hb[:, cols] = (a * jax.nn.sigmoid(a) * b).astype(BF)

            col_tiles(up)
            for q in (1, 2, 3):
                out_copy(q, f_bufs, slot).start()

            def down(cols):
                ob[:, cols] = dot(hb[...], wd[:, cols]).astype(BF)

            model_tiles(down)

            @pl.when(j == 0)
            def _():
                pltpu.make_async_copy(ob, back_o.at[rows_of(me)], outsem.at[4]).start()

            @pl.when(j > 0)
            def _():
                out_copy(4, f_bufs, slot).start()

        @pl.when(jnp.logical_not(is_f))
        def _():
            fetch(gy_ref, gyg, xbuf, lsem.at[0])
            fill_p()
            settle(i)
            load_a = pltpu.make_async_copy(a_out.at[rows_of(slot)], ab_a, lsem.at[2])
            load_b = pltpu.make_async_copy(b_out.at[rows_of(slot)], ab_b, lsem.at[3])
            load_a.start()
            load_b.start()
            g = jnp.sum(pbuf[...].astype(F32) * gate, axis=1, keepdims=True)
            fetched(gy_ref, xbuf, lsem.at[0])

            def pick(cols):
                cb[:, cols] = (g * dot(pbuf[...], xbuf[:, cols])).astype(BF)

            model_tiles(pick)
            out_copy(0, b_bufs, slot).start()
            load_a.wait()
            load_b.wait()

            def down_t(cols):
                dh = dot(cb[...], wd[cols, :], LAST).astype(BF).astype(F32)
                a, b = ab_a[:, cols], ab_b[:, cols]
                s = jax.nn.sigmoid(a)
                dab[:, cols] = (dh * b * (s * (1.0 + a * (1.0 - s)))).astype(BF)
                dbb[:, cols] = (dh * (a * s)).astype(BF)

            col_tiles(down_t)
            out_copy(1, b_bufs, slot).start()
            out_copy(2, b_bufs, slot).start()

            def up_t(cols):
                ob[:, cols] = (dot(dab[...], wg[cols, :], LAST) + dot(dbb[...], wu[cols, :], LAST)).astype(BF)

            model_tiles(up_t)
            out_copy(3, b_bufs, slot).start()

        return carry

    lax.fori_loop(0, 2 * n, step, 0)
    settle(2 * n)
    for j in range(1, n):
        taken(j)
        give(j).wait_send()
    for item in range(3):
        for k in range(8):
            if (item, k) != (2, 4):
                send(item, k).wait_send()


def layer(n, cap, x, gy, meta, w_gate, w_up, w_down):
    tok, d = x.shape
    ff = w_down.shape[1]
    rows = n * cap
    hbm = pl.BlockSpec(memory_space=pltpu.HBM)
    shapes = [
        ((rows, d), BF), ((rows, ff), F32), ((rows, ff), F32), ((rows, ff), BF), ((rows, d), BF), ((rows, d), BF),
        ((rows, ff), BF), ((rows, ff), BF), ((rows, d), BF), ((rows, d), BF),
        ((n, tok, d), BF), ((n, tok, d), BF), ((n, 8, tok), F32)]
    dma = pltpu.SemaphoreType.DMA
    return pl.pallas_call(
        functools.partial(layer_kernel, n, cap),
        out_shape=[jax.ShapeDtypeStruct(s, t) for s, t in shapes],
        in_specs=[hbm] * 6,
        out_specs=[hbm] * len(shapes),
        scratch_shapes=[
            pltpu.VMEM((d, ff), BF),
            pltpu.VMEM((d, ff), BF),
            pltpu.VMEM((ff, d), BF),
            pltpu.VMEM((tok, d), BF),
            pltpu.VMEM((8, tok), F32),
            pltpu.VMEM((tok, tok), BF),
            pltpu.VMEM((cap, tok), BF),
            pltpu.VMEM((n, 8, tok), jnp.int32),
            pltpu.VMEM((cap, d), BF),
            pltpu.VMEM((cap, ff), F32),
            pltpu.VMEM((cap, ff), F32),
            pltpu.VMEM((cap, ff), BF),
            pltpu.VMEM((cap, d), BF),
            pltpu.VMEM((cap, d), BF),
            pltpu.VMEM((cap, ff), BF),
            pltpu.VMEM((cap, ff), BF),
            dma((3, 8)), dma((3, 8)), dma((n,)), dma((n,)), dma((3,)), dma((4,)), dma((9,)),
        ],
        compiler_params=pltpu.CompilerParams(collective_id=0, has_side_effects=True, vmem_limit_bytes=62 * 1024 * 1024),
        cost_estimate=pl.CostEstimate(flops=2 * rows * d * (6 * ff + 2 * tok), bytes_accessed=700 * 1024 * 1024, transcendentals=2 * rows * ff),
        name="layer",
    )(x, gy, meta, w_gate, w_up, w_down)


def combine_kernel(n, back_ref, pos_ref, gate_ref, out_ref, acc):
    e = pl.program_id(0)
    tok = pos_ref.shape[0]
    cap, d = back_ref.shape[1:]
    lane = lax.broadcasted_iota(jnp.int32, (tok, n), 1)
    pos = jnp.sum(jnp.where(lane == e, pos_ref[...], 0), axis=1, keepdims=True)
    gate = jnp.sum(jnp.where(lane == e, gate_ref[...], 0.0), axis=1, keepdims=True)
    sel = jnp.where(lax.broadcasted_iota(jnp.int32, (tok, cap), 1) == pos, 1.0, 0.0).astype(BF)

    @pl.when(e == 0)
    def _():
        acc[...] = jnp.zeros_like(acc)

    def cols(m, c):
        at = pl.ds(pl.multiple_of(m * 512, 512), 512)
        acc[:, at] += gate * dot(sel, back_ref[0, :, at])
        return c

    lax.fori_loop(0, d // 512, cols, 0)

    @pl.when(e == n - 1)
    def _():
        out_ref[...] = acc[...].astype(BF)


def combine(n, back, pos, gate):
    tok = pos.shape[0]
    cap, d = back.shape[0] // n, back.shape[1]
    return pl.pallas_call(
        functools.partial(combine_kernel, n),
        grid=(n,),
        in_specs=[pl.BlockSpec((1, cap, d), lambda e: (e, 0, 0)), pl.BlockSpec((tok, n), lambda e: (0, 0)), pl.BlockSpec((tok, n), lambda e: (0, 0))],
        out_specs=pl.BlockSpec((tok, d), lambda e: (0, 0)),
        out_shape=jax.ShapeDtypeStruct((tok, d), BF),
        scratch_shapes=[pltpu.VMEM((tok, d), F32)],
        compiler_params=pltpu.CompilerParams(dimension_semantics=("arbitrary",), vmem_limit_bytes=48 * 1024 * 1024),
        cost_estimate=pl.CostEstimate(flops=2 * n * tok * cap * d, bytes_accessed=back.size * 2 + tok * d * 2, transcendentals=0),
        name="combine",
    )(back.reshape(n, cap, d), pos, gate)


def solution(mesh):
    n_exp = mesh.shape["ep"]
    row_spec = P(("dp", "ep"), None)
    weight_spec = P("ep", None, None)
    grad_w_spec = P(("dp", "ep"), None, None)

    def local(x, route_idx, route_gate, w_gate, w_up, w_down, grad_y):
        tok = x.shape[0]
        cap = 3 * tok // 4
        meta = jnp.concatenate([route_idx.astype(F32), route_gate], axis=1).T
        own = route_idx[:, :, None] == jnp.arange(n_exp, dtype=jnp.int32)
        own_hit = jnp.any(own, axis=1)
        own_gate = jnp.sum(jnp.where(own, route_gate[:, :, None], 0.0), axis=1)
        own_pos = jnp.where(own_hit, jnp.cumsum(own_hit.astype(jnp.int32), axis=0) - 1, -1)

        rows, _, _, h, _, c, da, db, r, back_o, _, _, _ = layer(n_exp, cap, x, grad_y, meta, w_gate, w_up, w_down)
        back_r = lax.all_to_all(r, "ep", 0, 0, tiled=True)
        gwg = dot(rows, da, FIRST).astype(BF)
        gwu = dot(rows, db, FIRST).astype(BF)
        gwd = dot(h, c, FIRST).astype(BF)
        y = combine(n_exp, back_o, own_pos, own_gate)
        grad_x = combine(n_exp, back_r, own_pos, jnp.ones_like(own_gate))
        return y, grad_x, gwg[None], gwu[None], gwd[None]

    return jax.shard_map(local, mesh=mesh, in_specs=(row_spec, row_spec, row_spec, weight_spec, weight_spec, weight_spec, row_spec), out_specs=(row_spec, row_spec, grad_w_spec, grad_w_spec, grad_w_spec), check_vma=False)
```

time: 1590 us -> 896 us (0.56)
  Pallas kernels: 0 us -> 644 us
  waiting for transfers between devices: 680 us -> 84.5 us
  local copies, waits for them, and re-layouts: 299 us -> 1 us
  matrix products: 439 us -> 144 us
  other arithmetic: 132 us -> 4.67 us
  starting transfers between devices: 27.8 us -> 6.8 us
    pallas_call x0 -> x3, Pallas kernels: none -> 644 us  [the longest x1 560 us: layer(): pl.pallas_call(functools.partial(layer_kernel, n, cap), out_shape=[jax.Sh...]
    all_to_all x4 -> x1, waiting for transfers between devices: 680 us -> 84.5 us  [local(): back_r = lax.all_to_all(r, 'ep', 0, 0, tiled=True)]
    dot_general x9 -> x3, matrix products: 439 us -> 144 us  [dot(): return lax.dot_general(a, b, dims, preferred_element_type=F32)]
    gather x4 -> x0, local copies, waits for them, and re-layouts: 184 us -> none  [the longest x1 49.1 us: local(): jnp.take(grad_y, src_tok, axis=0).astype(jnp.float32)]
    reduce_sum x3 -> x1, other arithmetic: 53.7 us -> 0.02 us  [local(): own_gate = jnp.sum(jnp.where(own, route_gate[:, :, None], 0.0), axis=1)]
    select_n x4 -> x1, other arithmetic: 51.5 us -> 0.06 us  [local(): jnp.where(own_hit, jnp.cumsum(own_hit.astype(jnp.int32), axis=0) - 1, -1)]
    scatter x3 -> x0, local copies, waits for them, and re-layouts: 48.8 us -> none  [the longest x1 17.7 us: pack_plan(): filled = jnp.zeros((n_dest * capacity,), jnp.bool_).at[slot_pos].set(True)]
    convert_element_type x1 -> x0, local copies, waits for them, and re-layouts: 37.4 us -> none  [local(): slot_out.astype(jnp.float32)]
  transfers between devices with their start and end apart: 4 -> 1, of which waited for: 4 -> 1; matrix products, arithmetic and copies ran while one was open for 26% -> 17% of each run, Pallas kernels for 0% -> 5%
where the time goes in v1:
time: 896 us; the launch traced here: 886 us
  Pallas kernels  644 us (72%)
  matrix products  144 us (16%)
  waiting for transfers between devices  84.5 us (9%)
    pallas_call x1, Pallas kernels, layer(): pl.pallas_call(functools.partial(layer_kernel, n, cap), out_shape=[jax.Sh...  560 us
    dot_general x3, matrix products, dot(): return lax.dot_general(a, b, dims, preferred_element_type=F32)  144 us
    all_to_all x1, waiting for transfers between devices, local(): back_r = lax.all_to_all(r, 'ep', 0, 0, tiled=True)  84.5 us
    pallas_call x2, Pallas kernels, combine(): pl.pallas_call(functools.partial(combine_kernel, n), grid=(n,), in_specs=...  84.4 us
  transfers between devices with their start and end apart: 1, of which 1 were waited for; matrix products, arithmetic and copies ran while one was open for 17% of the time, Pallas kernels for 5%

profile of v1, /device:TPU:112, one launch (start us, length us, event | category | flops | bytes accessed | tf_op | source)
XLA Modules:
  0.0 886.3 jit_solution(12861301097817104426)
XLA Ops:
  0.6 0.7 convert_element_type.17
  1.4 1.3 maximum_bitcast_fusion.meta_ref
  2.7 559.9 %layer.1 = (bf16[6144,2048]{1,0:T(8,128)(2,1)}, f32[6144,1408]{1,0:T(8,128)}, f32[6144,1408]{1,0:T(8,128)}, bf16[6144,1408]{1,0:T(8,128)(2,1)}, bf16[6144,2048]{...) custom-call(bf16[1024,2048]{1,0:T(8,128)(2,1)} %x_ref.1, ...), custom_call_target="tpu_custom_call" | custom-call | flops 264140488704 | bytes 734003200 | tf_op jit(solution)/shard_map/layer/pallas_call | solution.py:349
  562.6 0.0 copy-start
  562.6 0.0 copy-start.1
  562.6 6.8 all-to-all-start
  569.4 0.0 copy-done
  569.5 0.3 copy.22
  569.8 2.3 reduce-window.6
  572.0 0.3 slice_reduce_fusion
  572.3 0.2 reduce-window.9
  572.5 0.1 add_add_fusion
  572.6 0.2 copy.21
  572.8 0.0 copy-done.1
  572.8 0.2 copy.23.gate_ref
  573.0 0.1 bitcast_select_fusion.pos_ref
  573.1 42.2 %combine.2 = bf16[1024,2048]{1,0:T(8,128)(2,1)} custom-call(bf16[8,768,2048]{2,1,0:T(8,128)(2,1)} %bitcast.27, s32[1024,8]{1,0:T(8,128)S(1)} %bitcast_select_fusion.pos_ref, f32[1024,8]{1,0:T(8,128)S(1)} %copy.23.gate_ref), custom_call_target="tpu_custom_call" | custom-call | flops 25769803776 | bytes 29360128 | tf_op jit(solution)/shard_map/combine/pallas_call | solution.py:407
  615.3 48.9 %fusion.1 = bf16[1,2048,1408]{2,1,0:T(8,128)(2,1)} fusion(bf16[6144,2048]{1,0:T(8,128)(2,1)} %get-tuple-element.14, bf16[6144,1408]{1,0:T(8,128)(2,1)} %get-tuple-element.16), kind=kOutput, calls=%fused_computation.4 | convolution fusion | flops 35436363776 | bytes 48234496 | tf_op jit(solution)/shard_map/dot_general | solution.py:19
  664.2 49.1 %fusion = bf16[1,2048,1408]{2,1,0:T(8,128)(2,1)} fusion(bf16[6144,2048]{1,0:T(8,128)(2,1)} %get-tuple-element.14, bf16[6144,1408]{1,0:T(8,128)(2,1)} %get-tuple-element.15), kind=kOutput, calls=%fused_computation.3 | convolution fusion | flops 35436363776 | bytes 48234496 | tf_op jit(solution)/shard_map/dot_general | solution.py:19
  713.4 45.7 %fusion.2 = bf16[1,1408,2048]{2,1,0:T(8,128)(2,1)} fusion(bf16[6144,1408]{1,0:T(8,128)(2,1)} %get-tuple-element.17, bf16[6144,2048]{1,0:T(8,128)(2,1)} %get-tuple-element.18), kind=kOutput, calls=%fused_computation.5 | convolution fusion | flops 35436363776 | bytes 48234496 | tf_op jit(solution)/shard_map/dot_general | solution.py:19
  759.1 84.5 %all-to-all-done.back_ref = bf16[8,768,2048]{2,1,0:T(8,128)(2,1)} async-done(((bf16[8,768,2048]{2,1,0:T(8,128)(2,1)}), bf16[8,768,2048]{2,1,0:T(8,128)(2,1)}, u32[]{:S(2)}, u32[]{:S(2)}) %all-to-all-start) | async-done | bytes 25165856 | tf_op jit(solution)/shard_map/all_to_all | solution.py:436
  843.6 42.2 %combine.3 = bf16[1024,2048]{1,0:T(8,128)(2,1)} custom-call(bf16[8,768,2048]{2,1,0:T(8,128)(2,1)} %all-to-all-done.back_ref, s32[1024,8]{1,0:T(8,128)S(1)} %bitcast_select_fusion.pos_ref, f32[1024,8]{1,0:T(8,128)S(1)} %broadcast_in_dim.31.gate_ref), custom_call_target="tpu_custom_call" | custom-call | flops 25769803776 | bytes 29360128 | tf_op jit(solution)/shard_map/combine/pallas_call | solution.py:407
  (5 shorter events, 0.1 us)
Async XLA Ops:
  562.6 6.8 copy-start
  562.6 10.2 %copy-start.1 = (f32[1024,4]{0,1:T(4,128)S(1)}, f32[1024,4]{0,1:T(4,128)}, u32[]{:S(2)}) copy-start(f32[1024,4]{0,1:T(4,128)} %param.9) | copy-start | bytes 49156
  562.6 281.0 %all-to-all-start = ((bf16[8,768,2048]{2,1,0:T(8,128)(2,1)}), bf16[8,768,2048]{2,1,0:T(8,128)(2,1)}, u32[]{:S(2)}, u32[]{:S(2)}) async-start(bf16[8,768,2048]{2,1,0:T(8,128)(2,1)} %bitcast.25), calls=%async_computation | async-start | bytes 50331648 | tf_op jit(solution)/shard_map/all_to_all | solution.py:436

commit v2 on v1

v2 whole, which is shorter than its diff:
```python
import functools

import jax
import jax.numpy as jnp
from jax import lax
from jax.experimental import pallas as pl
from jax.experimental.pallas import tpu as pltpu
from jax.sharding import PartitionSpec as P

MESH = pl.DeviceIdType.MESH
MID = (((1,), (0,)), ((), ()))
LAST = (((1,), (1,)), ((), ()))
FIRST = (((0,), (0,)), ((), ()))
BF = jnp.bfloat16
F32 = jnp.float32
FOLD_AT = 8


def dot(a, b, dims=MID):
    return lax.dot_general(a, b, dims, preferred_element_type=F32)


def iota(shape, dim):
    return lax.broadcasted_iota(jnp.int32, shape, dim)


def ones(mask):
    return jnp.where(mask, 1.0, 0.0)


def total(v, axis):
    return jnp.sum(v, axis=axis, keepdims=True)


def tile(t, size):
    return pl.ds(pl.multiple_of(t * size, size), size)


def layer_kernel(n, cap, x_ref, gy_ref, meta_ref, wg_ref, wu_ref, wd_ref,
                 y_out, gx_out, gwg_out, gwu_out, gwd_out, xr_out, a_out, b_out, h_out, o_out, c_out, da_out, db_out, r_out, back_o, back_r, fold_o, fold_r, sum_o, sum_r, part_o, part_r, xg, gyg, mg,
                 wg, wu, wd, xbuf, mbuf, tri, pbuf, posbuf, gatebuf, xr, ab_a, ab_b, hb, ob, cb, dab, dbb, acc, lay, cols_own, cols_far,
                 send_sem, recv_sem, give_sem, take_sem, wsem, lsem, outsem, vsem):
    tok, d = x_ref.shape
    ff = wd_ref.shape[1]
    half = tok // 2
    me = lax.axis_index("ep")
    chips = n // 2
    chip, core = me // 2, lax.rem(me, 2)
    right = lax.rem(chip + 1, chips) * 2 + core
    left = lax.rem(chip + chips - 1, chips) * 2 + core
    across = lax.rem(chip + 2, chips) * 2 + core
    mate = chip * 2 + 1 - core
    right_m = lax.rem(chip + 1, chips) * 2 + 1 - core
    left_m = lax.rem(chip + chips - 1, chips) * 2 + 1 - core
    across_m = lax.rem(chip + 2, chips) * 2 + 1 - core
    lean = lax.rem(1 - 2 * core + chips, chips)
    ahead = lax.rem(chip + lean, chips) * 2 + core
    behind = lax.rem(chip + chips - lean, chips) * 2 + core
    ahead_m = lax.rem(chip + lean, chips) * 2 + 1 - core
    behind_m = lax.rem(chip + chips - lean, chips) * 2 + 1 - core
    peers = (left, right, mate, left_m, right_m)

    barrier = pltpu.get_barrier_semaphore()
    for peer in peers:
        pl.semaphore_signal(barrier, inc=1, device_id={"ep": peer}, device_id_type=MESH)
    pl.semaphore_wait(barrier, len(peers))

    own = (x_ref, gy_ref, meta_ref)
    got = (xg, gyg, mg)

    def whole(item, slot):
        return got[item].at[slot]

    def part(item, slot, which):
        return got[item].at[slot, pl.ds(which * half, half)] if item < 2 else got[item].at[slot]

    def mine(item, which):
        return own[item].at[pl.ds(which * half, half)] if item == 1 else own[item]

    def leg(item, k):
        beside = part if item == 1 else lambda i, slot, which: got[i].at[slot]
        return (
            (mine(item, 0), beside(item, me, 0), right, beside(item, left, 0)),
            (mine(item, 0), beside(item, me, 0), left, beside(item, right, 0)),
            (own[item], whole(item, me), mate, whole(item, mate)),
            (part(item, left, 0), part(item, left, 0), right, part(item, across, 0)),
            (part(item, right, 1), part(item, right, 1), left, part(item, across, 1)),
            (whole(item, left), whole(item, left), mate, whole(item, left_m)),
            (whole(item, right), whole(item, right), mate, whole(item, right_m)),
            (whole(item, across), whole(item, across), mate, whole(item, across_m)),
            (mine(item, 1), part(item, me, 1), right, part(item, left, 1)),
            (mine(item, 1), part(item, me, 1), left, part(item, right, 1)),
        )[k]

    def remote(src, dst, out_sem, in_sem, peer):
        return pltpu.make_async_remote_copy(
            src_ref=src, dst_ref=dst, send_sem=out_sem, recv_sem=in_sem, device_id={"ep": peer}, device_id_type=MESH)

    def send(item, k):
        src, dst, peer, _ = leg(item, k)
        return remote(src, dst, send_sem.at[item, k], recv_sem.at[item, k], peer)

    def start(item, *ks):
        for k in ks:
            send(item, k).start()

    def land(item, *ks):
        for k in ks:
            ref = leg(item, k)[-1]
            remote(ref, ref, send_sem.at[item, k], recv_sem.at[item, k], mate).wait_recv()

    def rows_of(slot):
        return tile(slot, cap)

    made, back, fold = (o_out, r_out), (back_o, back_r), (fold_o, fold_r)
    sums, parts = (sum_o, sum_r), (part_o, part_r)
    piece = tok // 4
    routes = ((mate, mate), (behind, behind), (ahead_m, ahead_m), (behind_m, mate), (across, ahead), (across_m, behind_m))
    sources = (mate, ahead, ahead_m)

    def give(w, k):
        rows, peer = routes[k]
        dst = back[w].at[rows_of(me)] if k < 3 else fold[w].at[k - 3]
        return remote(made[w].at[rows_of(rows)], dst, give_sem.at[w, k], take_sem.at[w, k], peer)

    def give_sum(w, q):
        at = pl.ds(q * piece, piece)
        return remote(sums[w].at[at], parts[w].at[at], give_sem.at[w, 6 + q], take_sem.at[w, 6 + q], ahead)

    def take(w, k):
        ref = back[w].at[rows_of(sources[k])] if k < 3 else fold[w].at[k - 3] if k < 6 else parts[w].at[pl.ds((k - 6) * piece, piece)]
        remote(ref, ref, give_sem.at[w, k], take_sem.at[w, k], mate).wait_recv()

    start(2, 0, 1, 2)
    start(0, 0, 1, 2)
    start(1, 0, 1, 2)

    weights = [pltpu.make_async_copy(s.at[0], t, wsem.at[q]) for q, (s, t) in enumerate(((wg_ref, wg), (wu_ref, wu), (wd_ref, wd)))]
    for cp in weights:
        cp.start()
    for q in range(4):
        band = (tok // 4, tok)
        tri[tile(q, tok // 4), :] = ones(iota(band, 0) + q * (tok // 4) <= iota(band, 1)).astype(BF)
    for cp in weights:
        cp.wait()

    def is_forward(i):
        return (i < 2) | ((i >= 4) & (i < 10))

    def slot_of(i):
        j = jnp.where(i < 2, i, jnp.where(i < 10, i - 2, i - 8))
        hop = jnp.where(j < 2, 0, jnp.where(j >= 6, 2, jnp.where(lax.rem(j, 2) == 0, lean, chips - lean)))
        flip = (j == 1) | (j == 4) | (j == 5) | (j == 7)
        return j, lax.rem(chip + hop, chips) * 2 + jnp.where(flip, 1 - core, core)

    f_bufs = ((xr, xr_out), (ab_a, a_out), (ab_b, b_out), (hb, h_out), (ob, o_out))
    b_bufs = ((cb, c_out), (dab, da_out), (dbb, db_out), (ob, r_out))

    def out_copy(q, bufs, slot):
        src, dst = bufs[q]
        return pltpu.make_async_copy(src, dst.at[rows_of(slot)], outsem.at[q + (5 if bufs is b_bufs else 0)])

    wide = ff // 256
    rest = pl.ds(wide * 256, ff % 256)

    def loop(count, body):
        def run(t, c):
            body(t)
            return c

        lax.fori_loop(0, count, run, 0)

    def col_tiles(body):
        loop(wide, lambda t: body(tile(t, 256)))
        if ff % 256:
            body(rest)

    def model_tiles(body):
        loop(d // 512, lambda t: body(tile(t, 512)))

    def settle(i):
        last = i - 1

        @pl.when((i > 0) & is_forward(last))
        def _():
            for q in range(5):
                out_copy(q, f_bufs, 0).wait()

        @pl.when((i > 0) & jnp.logical_not(is_forward(last)))
        def _():
            for q in range(4):
                out_copy(q, b_bufs, 0).wait()

        for when, w, sends in (
            (2, 0, (0,)), (4, 1, (0,)), (7, 0, (1, 2)), (8, 0, (3,)), (9, 0, (4,)), (10, 0, (5,)),
            (12, 1, (1,)), (13, 1, (2,)), (14, 1, (3,)), (15, 1, (4,)), (16, 1, (5,))):
            @pl.when(i == when)
            def _(w=w, sends=sends):
                for k in sends:
                    give(w, k).start()

    def step(i):
        is_f = is_forward(i)
        j, slot = slot_of(i)

        def at(when):
            return pl.when(i == when)

        @at(1)
        def _():
            land(2, 2)
            land(0, 2)

        @at(3)
        def _():
            land(1, 2)
            land(2, 0, 1)
            land(0, 0, 1)
            start(2, 3, 5, 6)
            start(0, 3, 4, 5, 6)
            start(1, 8, 9)

        @at(6)
        def _():
            land(2, 5, 6)
            land(0, 5, 6)

        @at(8)
        def _():
            land(2, 3)
            land(0, 3, 4)
            start(2, 7)
            start(0, 7)
            land(1, 0, 1, 8, 9)
            start(1, 3, 4, 5, 6)

        @at(9)
        def _():
            land(2, 7)
            land(0, 7)

        @at(12)
        def _():
            land(1, 5, 6)

        @at(14)
        def _():
            land(1, 3, 4)
            start(1, 7)

        @at(15)
        def _():
            land(1, 7)

        def fetch(own_ref, got_ref, buf, sem):
            @pl.when(j == 0)
            def _():
                pltpu.make_async_copy(own_ref, buf, sem).start()

            @pl.when(j > 0)
            def _():
                pltpu.make_async_copy(got_ref.at[slot], buf, sem).start()

        def fetched(own_ref, buf, sem):
            pltpu.make_async_copy(own_ref, buf, sem).wait()

        def fill_p():
            pos = posbuf[j][0:1, :]
            for q in range(cap // 128):
                pbuf[tile(q, 128), :] = ones(iota((128, tok), 0) + q * 128 == pos).astype(BF)

        @pl.when(is_f)
        def _():
            fetch(meta_ref, mg, mbuf, lsem.at[1])
            fetch(x_ref, xg, xbuf, lsem.at[0])
            fetched(meta_ref, mbuf, lsem.at[1])
            sel = mbuf[0:4, :] == me.astype(F32)
            gatebuf[j] = jnp.broadcast_to(total(jnp.where(sel, mbuf[4:8, :], 0.0), 0), (8, tok))
            hit = total(ones(sel), 0)
            count = dot(jnp.broadcast_to(hit, (16, tok)).astype(BF), tri[:])[0:1, :]
            pos = jnp.where(hit > 0.0, count - 1.0, -1.0).astype(jnp.int32)
            posbuf[j] = jnp.broadcast_to(pos, (8, tok))
            fill_p()
            settle(i)
            fetched(x_ref, xbuf, lsem.at[0])

            def pick(cols):
                xr[:, cols] = dot(pbuf[:], xbuf[:, cols]).astype(BF)

            model_tiles(pick)
            out_copy(0, f_bufs, slot).start()

            def up(cols):
                a, b = dot(xr[:], wg[:, cols]), dot(xr[:], wu[:, cols])
                ab_a[:, cols] = a
                ab_b[:, cols] = b
                hb[:, cols] = (a * jax.nn.sigmoid(a) * b).astype(BF)

            col_tiles(up)
            for q in (1, 2, 3):
                out_copy(q, f_bufs, slot).start()

            def down(cols):
                ob[:, cols] = dot(hb[:], wd[:, cols]).astype(BF)

            model_tiles(down)

            @pl.when(j == 0)
            def _():
                pltpu.make_async_copy(ob, back_o.at[rows_of(me)], outsem.at[4]).start()

            @pl.when(j > 0)
            def _():
                out_copy(4, f_bufs, slot).start()

        @pl.when(jnp.logical_not(is_f))
        def _():
            fetch(gy_ref, gyg, xbuf, lsem.at[0])
            fill_p()
            settle(i)
            load_a = pltpu.make_async_copy(a_out.at[rows_of(slot)], ab_a, lsem.at[2])
            load_b = pltpu.make_async_copy(b_out.at[rows_of(slot)], ab_b, lsem.at[3])
            load_a.start()
            load_b.start()
            g = total(pbuf[:].astype(F32) * gatebuf[j][0:1, :], 1)
            fetched(gy_ref, xbuf, lsem.at[0])

            def pick(cols):
                cb[:, cols] = (g * dot(pbuf[:], xbuf[:, cols])).astype(BF)

            model_tiles(pick)
            out_copy(0, b_bufs, slot).start()
            load_a.wait()
            load_b.wait()

            def down_t(cols):
                dh = dot(cb[:], wd[cols, :], LAST).astype(BF).astype(F32)
                a, b = ab_a[:, cols], ab_b[:, cols]
                s = jax.nn.sigmoid(a)
                dab[:, cols] = (dh * b * (s * (1.0 + a * (1.0 - s)))).astype(BF)
                dbb[:, cols] = (dh * (a * s)).astype(BF)

            col_tiles(down_t)
            out_copy(1, b_bufs, slot).start()
            out_copy(2, b_bufs, slot).start()

            def up_t(cols):
                ob[:, cols] = (dot(dab[:], wg[cols, :], LAST) + dot(dbb[:], wu[cols, :], LAST)).astype(BF)

            model_tiles(up_t)

            @pl.when(j == 0)
            def _():
                pltpu.make_async_copy(ob, back_r.at[rows_of(me)], outsem.at[8]).start()

            @pl.when(j > 0)
            def _():
                out_copy(3, b_bufs, slot).start()

    loop(2 * n, step)
    settle(2 * n)

    def lay_out(meta_src, cols):
        cp = pltpu.make_async_copy(meta_src, mbuf, lsem.at[1])
        cp.start()
        cp.wait()
        which = iota((n, tok), 0).astype(F32)
        hit, gate = jnp.zeros((n, tok), F32), jnp.zeros((n, tok), F32)
        for k in range(4):
            match = mbuf[k:k + 1, :] == which
            hit = hit + ones(match)
            gate = gate + jnp.where(match, mbuf[4 + k:5 + k, :], 0.0)
        count = dot(jnp.concatenate([hit, hit], axis=0).astype(BF), tri[:])[0:n, :]
        lay[:] = jnp.zeros_like(lay)
        lay[0:n, :] = jnp.where(hit > 0.0, count - 1.0, -1.0)
        lay[n:2 * n, :] = gate
        cols[:] = lay[:].T

    lay_out(meta_ref, cols_own)
    lay_out(mg.at[ahead], cols_far)
    picked = xbuf.at[:, pl.ds(0, cap)]

    def gains(w, cols, experts, srcs, waits):
        acc[:] = jnp.zeros_like(acc)

        def gain(q):
            e = experts[0]
            for k in range(4):
                e = jnp.where(q == k, experts[k], e)

                @pl.when(q == k)
                def _(k=k):
                    if waits[k] is not None:
                        take(w, waits[k])
                    pltpu.make_async_copy(srcs[k], cb, lsem.at[0]).start()

            lane = iota((tok, 128), 1)

            def column(k):
                return total(jnp.where(lane == k, cols[:], 0.0), 1)

            picked[:] = ones(iota((tok, cap), 1) == column(e).astype(jnp.int32)).astype(BF)
            gate = column(e + n) if w == 0 else 1.0
            pltpu.make_async_copy(srcs[0], cb, lsem.at[0]).wait()

            def add(at):
                part = dot(picked[:], cb[:, at])
                acc[:, at] += gate * part

            model_tiles(add)

        loop(4, gain)

    def fold_up(w):
        gains(w, cols_far, (me, mate, behind, behind_m),
              (made[w].at[rows_of(ahead)], fold[w].at[0], fold[w].at[1], fold[w].at[2]), (None, 3, 4, 5))
        cp = pltpu.make_async_copy(acc, sums[w], lsem.at[1])
        cp.start()
        cp.wait()
        for q in range(4):
            give_sum(w, q).start()

    def finish(w, out):
        gains(w, cols_own, (me, mate, ahead, ahead_m),
              tuple(back[w].at[rows_of(e)] for e in (me, mate, ahead, ahead_m)), (None, 0, 1, 2))
        stores = []
        for q in range(4):
            at = pl.ds(q * piece, piece)
            take(w, 6 + q)
            halves = ((ab_a, 0), (ab_b, d // 2))
            loads = [pltpu.make_async_copy(parts[w].at[at, pl.ds(c0, d // 2)], b.at[pl.ds(0, piece), pl.ds(0, d // 2)], vsem.at[2 + k])
                     for k, (b, c0) in enumerate(halves)]
            for cp in loads:
                cp.start()
            for cp in loads:
                cp.wait()
            for b, c0 in halves:
                cols = pl.ds(c0, d // 2)
                xbuf[at, cols] = (acc[at, cols] + b[pl.ds(0, piece), pl.ds(0, d // 2)]).astype(BF)
            stores.append(pltpu.make_async_copy(xbuf.at[at], out.at[at], outsem.at[3 + q]))
            stores[-1].start()
        for cp in stores:
            cp.wait()

    fold_up(0)

    for f0, fn in ((0, cap), (cap, ff - cap)):
        d_bufs = ((hb.at[:, pl.ds(0, fn)], cb), (dab.at[:, pl.ds(0, fn)], xr))
        h_turned = ob.at[pl.ds(0, fn), pl.ds(0, cap)]
        stage_d = xbuf.at[pl.ds(0, fn), :]

        def d_load(blk, p, f0=f0, fn=fn, d_bufs=d_bufs):
            srcs = (h_out.at[rows_of(blk), pl.ds(f0, fn)], c_out.at[rows_of(blk)])
            return [pltpu.make_async_copy(a, b, vsem.at[p * 3 + q]) for q, (a, b) in enumerate(zip(srcs, d_bufs[p]))]

        def d_step(blk, p, fn=fn, d_bufs=d_bufs, h_turned=h_turned, d_load=d_load):
            @pl.when(blk + 1 < n)
            def _():
                for cp in d_load(blk + 1, 1 - p):
                    cp.start()

            for cp in d_load(blk, p):
                cp.wait()
            h_turned[:] = d_bufs[p][0][:].T

            @pl.when(blk == 0)
            def _():
                acc[pl.ds(0, fn), :] = jnp.zeros((fn, d), F32)

            def add(cols):
                acc[pl.ds(0, fn), cols] += dot(h_turned[:], d_bufs[p][1][:, cols])

            model_tiles(add)

        def d_pair(u, d_step=d_step):
            d_step(2 * u, 0)
            d_step(2 * u + 1, 1)

        for cp in d_load(0, 0):
            cp.start()
        loop(n // 2, d_pair)
        stage_d[:] = acc[pl.ds(0, fn), :].astype(BF)
        store = pltpu.make_async_copy(stage_d, gwd_out.at[0, pl.ds(f0, fn)], outsem.at[2])
        store.start()
        store.wait()

    band = 512
    gu_bufs = ((pbuf.at[:, pl.ds(0, band)], dab, dbb), (pbuf.at[:, pl.ds(band, band)], hb, xbuf.at[pl.ds(0, cap), pl.ds(0, ff)]))
    stage_g, stage_u = ob.at[pl.ds(0, band), pl.ds(0, ff)], xr.at[pl.ds(0, band), pl.ds(0, ff)]
    turned = cb.at[pl.ds(0, band), pl.ds(0, cap)]

    def gu_load(t, p):
        m, blk = t // n, lax.rem(t, n)
        srcs = (xr_out.at[rows_of(blk), pl.ds(pl.multiple_of(m * band, band), band)], da_out.at[rows_of(blk)], db_out.at[rows_of(blk)])
        return [pltpu.make_async_copy(a, b, vsem.at[p * 3 + q]) for q, (a, b) in enumerate(zip(srcs, gu_bufs[p]))]

    def gu_store(m):
        at = pl.ds(pl.multiple_of(m * band, band), band)
        return [pltpu.make_async_copy(stage_g, gwg_out.at[0, at], outsem.at[0]), pltpu.make_async_copy(stage_u, gwu_out.at[0, at], outsem.at[1])]

    def gu_step(t, p):
        @pl.when(t + 1 < (d // band) * n)
        def _():
            for cp in gu_load(t + 1, 1 - p):
                cp.start()

        for cp in gu_load(t, p):
            cp.wait()
        xt, g_blk, u_blk = gu_bufs[p]
        turned[:] = xt[:].T

        @pl.when(lax.rem(t, n) == 0)
        def _():
            acc[:, pl.ds(0, ff)] = jnp.zeros((2 * band, ff), F32)

        def add(cols):
            acc[pl.ds(0, band), cols] += dot(turned[:], g_blk[:, cols])
            acc[pl.ds(band, band), cols] += dot(turned[:], u_blk[:, cols])

        col_tiles(add)

    def gu_pair(u):
        @pl.when(u == FOLD_AT)
        def _():
            fold_up(1)

        gu_step(2 * u, 0)
        gu_step(2 * u + 1, 1)
        m = (2 * u + 1) // n

        @pl.when(lax.rem(2 * u + 1, n) == n - 1)
        def _():
            @pl.when(m > 0)
            def _():
                for cp in gu_store(0):
                    cp.wait()

            stage_g[:] = acc[pl.ds(0, band), pl.ds(0, ff)].astype(BF)
            stage_u[:] = acc[pl.ds(band, band), pl.ds(0, ff)].astype(BF)
            for cp in gu_store(m):
                cp.start()

    for cp in gu_load(0, 0):
        cp.start()
    loop((d // band) * n // 2, gu_pair)
    for cp in gu_store(0):
        cp.wait()

    finish(0, y_out)
    finish(1, gx_out)
    for w in range(2):
        for k in range(len(routes)):
            give(w, k).wait_send()
        for q in range(4):
            give_sum(w, q).wait_send()
    for item, ks in enumerate((range(8), range(10), (0, 1, 2, 3, 5, 6, 7))):
        for k in ks:
            send(item, k).wait_send()


def layer(n, cap, x, gy, meta, w_gate, w_up, w_down):
    tok, d = x.shape
    ff = w_down.shape[1]
    rows = n * cap
    hbm = pl.BlockSpec(memory_space=pltpu.HBM)
    shapes = [
        ((tok, d), BF), ((tok, d), BF), ((1, d, ff), BF), ((1, d, ff), BF), ((1, ff, d), BF),
        ((rows, d), BF), ((rows, ff), F32), ((rows, ff), F32), ((rows, ff), BF), ((rows, d), BF), ((rows, d), BF),
        ((rows, ff), BF), ((rows, ff), BF), ((rows, d), BF), ((rows, d), BF), ((rows, d), BF),
        ((3, cap, d), BF), ((3, cap, d), BF), ((tok, d), F32), ((tok, d), F32), ((tok, d), F32), ((tok, d), F32),
        ((n, tok, d), BF), ((n, tok, d), BF), ((n, 8, tok), F32)]
    dma = pltpu.SemaphoreType.DMA
    return pl.pallas_call(
        functools.partial(layer_kernel, n, cap),
        out_shape=[jax.ShapeDtypeStruct(s, t) for s, t in shapes],
        in_specs=[hbm] * 6,
        out_specs=[hbm] * len(shapes),
        scratch_shapes=[
            pltpu.VMEM((d, ff), BF),
            pltpu.VMEM((d, ff), BF),
            pltpu.VMEM((ff, d), BF),
            pltpu.VMEM((tok, d), BF),
            pltpu.VMEM((8, tok), F32),
            pltpu.VMEM((tok, tok), BF),
            pltpu.VMEM((cap, tok), BF),
            pltpu.VMEM((n, 8, tok), jnp.int32),
            pltpu.VMEM((n, 8, tok), F32),
            pltpu.VMEM((cap, d), BF),
            pltpu.VMEM((cap, ff), F32),
            pltpu.VMEM((cap, ff), F32),
            pltpu.VMEM((cap, ff), BF),
            pltpu.VMEM((cap, d), BF),
            pltpu.VMEM((cap, d), BF),
            pltpu.VMEM((cap, ff), BF),
            pltpu.VMEM((cap, ff), BF),
            pltpu.VMEM((tok, d), F32),
            pltpu.VMEM((128, tok), F32),
            pltpu.VMEM((tok, 128), F32),
            pltpu.VMEM((tok, 128), F32),
            dma((3, 10)), dma((3, 10)), dma((2, 10)), dma((2, 10)), dma((3,)), dma((4,)), dma((9,)), dma((6,)),
        ],
        compiler_params=pltpu.CompilerParams(collective_id=0, has_side_effects=True, vmem_limit_bytes=67043328),
        cost_estimate=pl.CostEstimate(flops=2 * rows * d * (6 * ff + 2 * tok), bytes_accessed=700 * 1024 * 1024, transcendentals=2 * rows * ff),
        name="layer",
    )(x, gy, meta, w_gate, w_up, w_down)


def solution(mesh):
    n_exp = mesh.shape["ep"]
    row_spec = P(("dp", "ep"), None)
    weight_spec = P("ep", None, None)
    grad_w_spec = P(("dp", "ep"), None, None)

    def local(x, route_idx, route_gate, w_gate, w_up, w_down, grad_y):
        tok = x.shape[0]
        cap = 3 * tok // 4
        meta = jnp.concatenate([route_idx.astype(F32), route_gate], axis=1).T
        return tuple(layer(n_exp, cap, x, grad_y, meta, w_gate, w_up, w_down)[:5])

    return jax.shard_map(local, mesh=mesh, in_specs=(row_spec, row_spec, row_spec, weight_spec, weight_spec, weight_spec, row_spec), out_specs=(row_spec, row_spec, grad_w_spec, grad_w_spec, grad_w_spec), check_vma=False)
```

time: 896 us -> 762 us (0.85)
  matrix products: 144 us -> 0 us
  Pallas kernels: 644 us -> 740 us
  waiting for transfers between devices: 84.5 us -> 0 us
  local copies, waits for them, and re-layouts: 1 us -> 17.6 us
    pallas_call x1, Pallas kernels: 560 us -> 740 us  [layer(): pl.pallas_call(functools.partial(layer_kernel, n, cap), out_shape=[jax.Sh...]
    dot_general x3 -> x0, matrix products: 144 us -> none  [dot(): return lax.dot_general(a, b, dims, preferred_element_type=F32)]
    all_to_all x1 -> x0, waiting for transfers between devices: 84.5 us -> none  [local(): back_r = lax.all_to_all(r, 'ep', 0, 0, tiled=True)]
    pallas_call x2 -> x0, Pallas kernels: 84.4 us -> none  [combine(): pl.pallas_call(functools.partial(combine_kernel, n), grid=(n,), in_specs=...]
    unnamed x4 -> x19, local copies, waits for them, and re-layouts: 0.01 us -> 17.6 us
  transfers between devices with their start and end apart: 1 -> 0, of which waited for: 1 -> 0; matrix products, arithmetic and copies ran while one was open for 17% -> 0% of each run, Pallas kernels for 5% -> 0%
where the time goes in v2:
time: 762 us; the launch traced here: 760 us
  Pallas kernels  740 us (97%)
  local copies, waits for them, and re-layouts  17.6 us (2%)
    pallas_call x1, Pallas kernels, layer(): pl.pallas_call(functools.partial(layer_kernel, n, cap), out_shape=[jax.Sh...  740 us
    unnamed x19, local copies, waits for them, and re-layouts  17.6 us

profile of v2, /device:TPU:112, one launch (start us, length us, event | category | flops | bytes accessed | tf_op | source)
XLA Modules:
  0.0 760.1 jit_solution(8583836491549579834)
XLA Ops:
  0.6 0.7 convert_element_type.3
  1.4 1.3 maximum_bitcast_fusion.meta_ref
  2.7 739.7 %layer.1 = (bf16[1024,2048]{1,0:T(8,128)(2,1)}, bf16[1024,2048]{1,0:T(8,128)(2,1)}, bf16[1,2048,1408]{2,1,0:T(8,128)(2,1)}, bf16[1,2048,1408]{2,1,0:T(8,128)(2,1...) custom-call(bf16[1024,2048]{1,0:T(8,128)(2,1)} %x_ref.1, ...), custom_call_target="tpu_custom_call" | custom-call | flops 264140488704 | bytes 734003200 | tf_op jit(solution)/shard_map/layer/pallas_call | solution.py:573
  742.4 0.0 copy-start
  742.4 0.0 slice-start.4
  742.5 0.0 slice-start.5
  742.5 0.0 slice-start.2
  742.5 5.1 copy.17
  747.5 0.0 copy-done
  747.5 0.0 slice-start.3
  747.5 2.1 copy.18
  749.7 0.0 slice-done.4
  749.7 0.8 slice-done.5
  750.5 0.0 slice-start
  750.5 2.9 copy.19
  753.4 0.0 slice-done.2
  753.4 1.0 slice-done.3
  754.4 0.0 slice-start.1
  754.4 2.6 copy.20
  757.0 0.0 slice-done
  757.0 0.5 slice-done.1
  757.5 2.5 copy.21
  (3 shorter events, 0.0 us)
Async XLA Ops:
  742.4 5.1 copy-start
  742.4 7.2 slice-start.4
  742.5 8.0 %slice-start.5 = ((s8[5767168]{0:T(1024)(128)(4,1)}), s8[1572864]{0:T(1024)(128)(4,1)S(1)}, s32[]{:S(2)}) async-start(s8[5767168]{0:T(1024)(128)(4,1)} %bitcast.6), calls=%async_computation.5 | async-start | bytes 3145728
  742.5 10.9 %slice-start.2 = ((s8[5767168]{0:T(1024)(128)(4,1)}), s8[4194304]{0:T(1024)(128)(4,1)S(1)}, s32[]{:S(2)}) async-start(s8[5767168]{0:T(1024)(128)(4,1)} %bitcast.4), calls=%async_computation.2 | async-start | bytes 8388608
  747.5 6.9 slice-start.3
  750.5 6.6 slice-start
  754.4 3.1 slice-start.1
